TPU v7x, 32 devices: a whole 2x2x4 slice. The times are simulated.
32 devices in a mesh: dp: 2 (over x), fsdp: 4 (over z), mp: 4 (over y, core).
Axes of the slice: x: 2, y: 2, z: 4, core: 2. Of those that a mesh axis runs over, the one named last changes fastest.
Arguments:
- gradients: bfloat16 [8, 12, 2, 256, 1024], P(('dp', 'fsdp'), None, None, None, 'mp'), may hold values from -6 to 6
- master: float32 [12, 2, 256, 1024], P(None, None, ('dp', 'fsdp'), 'mp'), may hold values from -0.375 to 0.375
- teacher: float32 [12, 2, 256, 1024], P(None, None, ('dp', 'fsdp'), 'mp'), may hold values from -0.375 to 0.375
- first_moment: float32 [12, 2, 256, 1024], P(None, None, ('dp', 'fsdp'), 'mp'), may hold values from -2.2888184e-05 to 2.2888184e-05
- second_moment: float32 [12, 2, 256, 1024], P(None, None, ('dp', 'fsdp'), 'mp'), may hold values from 0 to 1, as said below
- layer_rates: float32 [12], replicated, may hold values from 0.02 to 0.2
Outputs:
- master_new: float32 [12, 2, 256, 1024], P(None, None, ('dp', 'fsdp'), 'mp')
- teacher_new: float32 [12, 2, 256, 1024], P(None, None, ('dp', 'fsdp'), 'mp')
- first_new: float32 [12, 2, 256, 1024], P(None, None, ('dp', 'fsdp'), 'mp')
- second_new: float32 [12, 2, 256, 1024], P(None, None, ('dp', 'fsdp'), 'mp')
- student_weights: bfloat16 [12, 2, 256, 1024], P(None, None, None, 'mp')
- teacher_weights: bfloat16 [12, 2, 256, 1024], P(None, None, None, 'mp')
Inputs may be any that keep to these rules, and one draw needn't show every extreme that they name: `second_moment`: every entry is positive.
All inputs are finite; a program needn't handle non-finite values.
Results may differ from a plain program's by a relative error of at most 0.0004.
Values may be sent and summed in bfloat16 or wider, within the bound.
A program may use at most 64 MiB of HBM per device.

v0:
```python
import jax
import jax.numpy as jnp
from jax import lax
from jax.sharding import PartitionSpec as P

CLIP_NORM = 0.1
BETA_ONE = 0.9
BETA_TWO = 0.999
BIAS_ONE = 1.0 - 0.9**50 * 0.9**50
BIAS_TWO = 1.0 - 0.999**50 * 0.999**50
ADAM_EPS = 1e-08
DECAY = 0.05
EMA_KEEP = 0.95


def shards(gradients, master, teacher, first_moment, second_moment, layer_rates):
    own_grad = gradients[0].astype(jnp.float32)
    summed = lax.psum_scatter(own_grad, ("dp", "fsdp"), scatter_dimension=2, tiled=True)
    mean_grad = summed / (lax.axis_size("dp") * lax.axis_size("fsdp"))
    norm_sq = lax.psum(jnp.sum(mean_grad * mean_grad), ("dp", "fsdp", "mp"))
    clip_factor = jnp.minimum(1.0, CLIP_NORM / (jnp.sqrt(norm_sq) + 1e-06))
    clipped = clip_factor * mean_grad
    first_new = BETA_ONE * first_moment + (1.0 - BETA_ONE) * clipped
    second_new = BETA_TWO * second_moment + (1.0 - BETA_TWO) * clipped * clipped
    direction = first_new / BIAS_ONE / (jnp.sqrt(second_new / BIAS_TWO) + ADAM_EPS) + DECAY * master
    layer_rate = layer_rates[:, None, None, None]
    master_new = master - layer_rate * direction
    teacher_new = EMA_KEEP * teacher + (1.0 - EMA_KEEP) * master_new
    student_half = master_new.astype(jnp.bfloat16)
    teacher_half = teacher_new.astype(jnp.bfloat16)
    student_weights, teacher_weights = (
        lax.all_gather(student_half, ("dp", "fsdp"), axis=2, tiled=True),
        lax.all_gather(teacher_half, ("dp", "fsdp"), axis=2, tiled=True),
    )
    return (master_new, teacher_new, first_new, second_new, student_weights, teacher_weights)


def solution(mesh):
    placed = (
        P(("dp", "fsdp"), None, None, None, "mp"),
        P(None, None, ("dp", "fsdp"), "mp"),
        P(None, None, ("dp", "fsdp"), "mp"),
        P(None, None, ("dp", "fsdp"), "mp"),
        P(None, None, ("dp", "fsdp"), "mp"),
        P(),
    )
    return jax.shard_map(
        shards,
        mesh=mesh,
        in_specs=placed,
        out_specs=(
            P(None, None, ("dp", "fsdp"), "mp"),
            P(None, None, ("dp", "fsdp"), "mp"),
            P(None, None, ("dp", "fsdp"), "mp"),
            P(None, None, ("dp", "fsdp"), "mp"),
            P(None, None, None, "mp"),
            P(None, None, None, "mp"),
        ),
        check_vma=False,
    )
```

profile of v0, /device:TPU:0, one launch (start us, length us, event | category | flops | bytes accessed | tf_op | source)
XLA Modules:
  0.0 313.6 jit_solution(9749156798036131048)
XLA Ops:
  7.2 0.0 reduce-scatter.2.cloned.1.call-start
  7.2 5.3 %bitcast_convert_fusion = f32[12,2,256,256]{3,2,1,0:T(8,128)} fusion(bf16[1,12,2,256,256]{4,3,2,1,0:T(8,128)(2,1)} %param.6), kind=kLoop, calls=%fused_computation | loop fusion | flops 1572864 | bytes 9437184 | tf_op jit(solution)/shard_map/convert_element_type | solution.py:17
  12.5 0.0 copy-start.2
  12.5 0.0 copy-start.3
  12.5 0.0 copy-start.4
  12.5 0.0 copy-start.5
  12.5 0.0 reduce-scatter.2.cloned.1.call-update
  12.6 0.0 all-gather.5.cloned.1.call-start
  12.6 121.3 %reduce-scatter.2.cloned.1.call-done = f32[12,2,32,256]{3,2,1,0:T(8,128)} async-done(((f32[12,2,256,256]{3,2,1,0:T(8,128)}), f32[12,2,32,256]{3,2,1,0:T(8,128)}) %reduce-scatter.2.cloned.1.call-update) | async-done | bytes 786448 | tf_op jit(solution)/shard_map/reduce_scatter | solution.py:18
  133.9 1.9 multiply_reduce_fusion
  135.8 39.7 %psum.7 = f32[]{:T(128)} all-reduce(f32[]{:T(128)} %multiply_reduce_fusion), channel_id=1, replica_groups=mesh['dp'=2,'fsdp'=4,'mp'=4] {'dp','fsdp','mp'}, use_global_device_ids=true, to_apply=%region_2.0 | all-reduce | flops 1 | bytes 8 | tf_op jit(solution)/shard_map/psum | solution.py:20
  176.3 0.0 copy-done.2
  176.3 0.0 copy-done.3
  176.3 0.0 copy-done.4
  176.3 0.0 copy-done.5
  176.3 3.5 %fusion.1 = (bf16[12,2,32,256]{3,2,1,0:T(8,128)(2,1)}, f32[12,2,32,256]{3,2,1,0:T(8,128)}, f32[12,2,32,256]{3,2,1,0:T(8,128)S(1)}, f32[12,2,32,256]{3,2,1,0:T(8,128)}, f32[12,2,32,256]{3,2,1,0:T(8,128)}) fusion(f32[12,2,32,256]{3,2,1,0:T(8,128)S(1)} %copy-done.2, f32[12,2,32,256]{3,2,1,0:T(8,128)S(1)} %copy-done.3, f32[12]{0:T(128)S(1)} %copy-done.5, ...), kind=kLoop, calls=%fused_computation.7 | loop fusion | flops 3932160 | bytes 7471156 | tf_op jit(solution)/shard_map/convert_element_type | solution.py:30
  179.8 0.0 copy-start.1
  179.8 0.0 all-gather.5.cloned.1.call-update
  179.8 0.0 all-gather.3.cloned.1.call-start
  179.9 1.0 convert_element_type.14
  180.9 0.0 all-gather.3.cloned.1.call-update
  180.9 59.0 %all-gather.5.cloned.1.call-done = bf16[12,2,256,256]{3,2,1,0:T(8,128)(2,1)} async-done(((bf16[12,2,32,256]{3,2,1,0:T(8,128)(2,1)}), bf16[12,2,256,256]{3,2,1,0:T(8,128)(2,1)}) %all-gather.5.cloned.1.call-update) | async-done | bytes 3145744 | tf_op jit(solution)/shard_map/all_gather | solution.py:33
  239.9 61.5 %all-gather.3.cloned.1.call-done = bf16[12,2,256,256]{3,2,1,0:T(8,128)(2,1)} async-done(((bf16[12,2,32,256]{3,2,1,0:T(8,128)(2,1)}), bf16[12,2,256,256]{3,2,1,0:T(8,128)(2,1)}) %all-gather.3.cloned.1.call-update) | async-done | bytes 3145744 | tf_op jit(solution)/shard_map/all_gather | solution.py:32
  301.4 0.0 copy-start
  301.4 4.0 %copy.14 = bf16[12,2,256,256]{3,2,1,0:T(8,128)(2,1)} copy(bf16[12,2,256,256]{3,2,1,0:T(8,128)(2,1)} %all-gather.3.cloned.1.call-done) | data formatting | bytes 6291456
  305.4 0.0 copy-done.1
  305.4 0.0 copy-done
  305.4 1.7 copy.15
Async XLA Ops:
  7.2 126.7 %reduce-scatter.2.cloned.1.call-start = ((), (), s32[]{:S(2)}) async-start(), calls=%async_computation.1 | async-start | bytes 7077888 | tf_op jit(solution)/shard_map/reduce_scatter | solution.py:18
  12.5 163.8 %copy-start.2 = (f32[12,2,32,256]{3,2,1,0:T(8,128)S(1)}, f32[12,2,32,256]{3,2,1,0:T(8,128)}, u32[]{:S(2)}) copy-start(f32[12,2,32,256]{3,2,1,0:T(8,128)} %param.8) | copy-start | bytes 2359300
  12.5 163.8 %copy-start.3 = (f32[12,2,32,256]{3,2,1,0:T(8,128)S(1)}, f32[12,2,32,256]{3,2,1,0:T(8,128)}, u32[]{:S(2)}) copy-start(f32[12,2,32,256]{3,2,1,0:T(8,128)} %param.7) | copy-start | bytes 2359300
  12.5 163.8 %copy-start.4 = (f32[12,2,32,256]{3,2,1,0:T(8,128)S(1)}, f32[12,2,32,256]{3,2,1,0:T(8,128)}, u32[]{:S(2)}) copy-start(f32[12,2,32,256]{3,2,1,0:T(8,128)} %param.9) | copy-start | bytes 2359300
  12.5 163.8 %copy-start.5 = (f32[12]{0:T(128)S(1)}, f32[12]{0:T(128)}, u32[]{:S(2)}) copy-start(f32[12]{0:T(128)} %param.11) | copy-start | bytes 148
  12.6 227.4 %all-gather.5.cloned.1.call-start = ((), (), s32[]{:S(2)}) async-start(), calls=%async_computation.3 | async-start | bytes 3538944 | tf_op jit(solution)/shard_map/all_gather | solution.py:33
  179.8 125.6 %copy-start.1 = (f32[12,2,32,256]{3,2,1,0:T(8,128)}, f32[12,2,32,256]{3,2,1,0:T(8,128)S(1)}, u32[]{:S(2)}) copy-start(f32[12,2,32,256]{3,2,1,0:T(8,128)S(1)} %get-tuple-element.17) | copy-start | bytes 2359300
  179.8 121.6 %all-gather.3.cloned.1.call-start = ((), (), s32[]{:S(2)}) async-start(), calls=%async_computation.2 | async-start | bytes 3538944 | tf_op jit(solution)/shard_map/all_gather | solution.py:32
  301.4 4.0 %copy-start = (bf16[12,2,256,256]{3,2,1,0:T(8,128)(2,1)S(1)}, bf16[12,2,256,256]{3,2,1,0:T(8,128)(2,1)}, u32[]{:S(2)}) copy-start(bf16[12,2,256,256]{3,2,1,0:T(8,128)(2,1)} %all-gather.5.cloned.1.call-done) | copy-start | bytes 9437188
Sparse Core Ops, SparseCore 0:
  12.7 121.1 reduce-scatter.1
  180.0 59.9 all-gather.4
  242.7 58.6 all-gather.2
where the time goes:
time: 314 us
  waiting for transfers between devices  242 us (77%)
  blocking collectives  39.7 us (13%)
  between operations  14.5 us (5%)
  other arithmetic  11.7 us (4%)
  local copies, waits for them, and re-layouts  5.69 us (2%)
    reduce_scatter x1, waiting for transfers between devices, shards(): lax.psum_scatter(own_grad, ('dp', 'fsdp'), scatter_dimension=2, tiled=True)  121 us
    all_gather x1, waiting for transfers between devices, shards(): lax.all_gather(student_half, ('dp', 'fsdp'), axis=2, tiled=True)  61.5 us
    all_gather x1, waiting for transfers between devices, shards(): lax.all_gather(teacher_half, ('dp', 'fsdp'), axis=2, tiled=True)  59 us
    psum x1, blocking collectives, shards(): norm_sq = lax.psum(jnp.sum(mean_grad * mean_grad), ('dp', 'fsdp', 'mp'))  39.7 us
  transfers between devices with their start and end apart: 3, of which 3 were waited for; matrix products, arithmetic and copies ran while one was open for 0% of the time, Pallas kernels for 0%

commit v1 on v0

v1 whole, which is shorter than its diff:
```python
import functools
import math

import jax
import jax.numpy as jnp
from jax import lax
from jax.experimental import pallas as pl
from jax.experimental.pallas import tpu as pltpu
from jax.sharding import PartitionSpec as P

CLIP_NORM = 0.1
BETA_ONE = 0.9
BETA_TWO = 0.999
BIAS_ONE = 1.0 - 0.9**50 * 0.9**50
BIAS_TWO = 1.0 - 0.999**50 * 0.999**50
ADAM_EPS = 1e-08
DECAY = 0.05
EMA_KEEP = 0.95
MESH = pl.DeviceIdType.MESH


def updated(mean_grad, clip_factor, master, teacher, first_moment, second_moment, layer_rate):
    clipped = clip_factor * mean_grad
    first_new = BETA_ONE * first_moment + (1.0 - BETA_ONE) * clipped
    second_new = BETA_TWO * second_moment + (1.0 - BETA_TWO) * clipped * clipped
    direction = first_new / BIAS_ONE / (jnp.sqrt(second_new / BIAS_TWO) + ADAM_EPS) + DECAY * master
    master_new = master - layer_rate * direction
    teacher_new = EMA_KEEP * teacher + (1.0 - EMA_KEEP) * master_new
    return master_new, teacher_new, first_new, second_new


def plain_shards(gradients, master, teacher, first_moment, second_moment, layer_rates):
    own_grad = gradients[0].astype(jnp.float32)
    summed = lax.psum_scatter(own_grad, ("dp", "fsdp"), scatter_dimension=2, tiled=True)
    mean_grad = summed / (lax.axis_size("dp") * lax.axis_size("fsdp"))
    norm_sq = lax.psum(jnp.sum(mean_grad * mean_grad), ("dp", "fsdp", "mp"))
    clip_factor = jnp.minimum(1.0, CLIP_NORM / (jnp.sqrt(norm_sq) + 1e-06))
    layer_rate = layer_rates[:, None, None, None]
    new = updated(mean_grad, clip_factor, master, teacher, first_moment, second_moment, layer_rate)
    student_half, teacher_half = new[0].astype(jnp.bfloat16), new[1].astype(jnp.bfloat16)
    return (
        *new,
        lax.all_gather(student_half, ("dp", "fsdp"), axis=2, tiled=True),
        lax.all_gather(teacher_half, ("dp", "fsdp"), axis=2, tiled=True),
    )


def step_kernel(
    sizes, chunks, grad, master, teacher, first, second, rates,
    master_out, teacher_out, first_out, second_out, student_w, teacher_w,
    own, met, mean, state, fresh, half, norm_own, norm_met,
    own_sem, state_sem, out_sem, half_sem,
    a_send, a_recv, n_send, n_recv, g_send, g_recv, f_send, f_recv,
):
    nd, nf, nm = sizes
    x, z, m = lax.axis_index("dp"), lax.axis_index("fsdp"), lax.axis_index("mp")
    slabs, rows, width = mean.shape
    per = slabs // chunks
    halves = slabs // rates.shape[0]
    total = nd * nf
    place = pl.ds(pl.multiple_of((x * nf + z) * rows, rows), rows)
    cut = [pl.ds(k * per, per) for k in range(chunks)]
    peers = [(a, b) for a in range(nd) for b in range(nf) if (a, b) != (0, 0)]

    def at_x(a):
        return lax.rem(x + a, nd)

    def at_z(b):
        return lax.rem(z + b, nf)

    def at_m(c):
        return lax.rem(m + c, nm)

    def remote(src, dst, send, recv, **where):
        return pltpu.make_async_remote_copy(
            src_ref=src, dst_ref=dst, send_sem=send, recv_sem=recv, device_id=where, device_id_type=MESH
        )

    barrier = pltpu.get_barrier_semaphore()
    for a, b in peers:
        pl.semaphore_signal(barrier, inc=1, device_id={"dp": at_x(a), "fsdp": at_z(b)}, device_id_type=MESH)
    for c in range(1, nm):
        pl.semaphore_signal(barrier, inc=1, device_id={"mp": at_m(c)}, device_id_type=MESH)

    takes = [pltpu.make_async_copy(grad.at[cut[k], place, :], own.at[cut[k]], own_sem.at[k]) for k in range(chunks)]
    for take in takes:
        take.start()
    loads = [pltpu.make_async_copy(ref, state.at[i], state_sem.at[i]) for i, ref in enumerate((master, teacher, first, second))]
    pl.semaphore_wait(barrier, len(peers) + nm - 1)

    sent = {}
    for k in range(chunks):
        for i, (a, b) in enumerate(peers):
            theirs = pl.ds(pl.multiple_of((at_x(a) * nf + at_z(b)) * rows, rows), rows)
            sent[k, i] = remote(
                grad.at[cut[k], theirs, :], met.at[i, cut[k]], a_send.at[i, k], a_recv.at[i, k], dp=at_x(a), fsdp=at_z(b)
            )
            sent[k, i].start()
    for load in loads:
        load.start()

    square = jnp.zeros((8, 128), jnp.float32)
    for k in range(chunks):
        takes[k].wait()
        for i in range(len(peers)):
            sent[k, i].wait_recv()
        for s in range(k * per, (k + 1) * per):
            value = own[s].astype(jnp.float32)
            for i in range(len(peers)):
                value = value + met[i, s].astype(jnp.float32)
            value = value / total
            mean[s] = value
            for part in range(width // 128):
                lane = value[:, part * 128:(part + 1) * 128]
                square = square + jnp.sum((lane * lane).reshape(-1, 8, 128), axis=0)

    norm_own[0] = square
    told = []
    for i, (a, b) in enumerate(peers):
        told.append(remote(norm_own.at[0], norm_met.at[i], n_send.at[i], n_recv.at[i], dp=at_x(a), fsdp=at_z(b)))
        told[-1].start()
    for load in loads:
        load.wait()
    for i in range(len(peers)):
        told[i].wait_recv()
        square = square + norm_met[i]
    norm_own[1] = square
    for c in range(1, nm):
        i = len(peers) + c - 1
        told.append(remote(norm_own.at[1], norm_met.at[i], n_send.at[i], n_recv.at[i], mp=at_m(c)))
        told[-1].start()
    for c in range(1, nm):
        i = len(peers) + c - 1
        told[i].wait_recv()
        square = square + norm_met[i]
    norm_sq = jnp.sum(jnp.sum(square, axis=0, keepdims=True), axis=1, keepdims=True)
    clip_factor = jnp.minimum(1.0, CLIP_NORM / (jnp.sqrt(norm_sq) + 1e-06))

    weights = (student_w, teacher_w)
    spread, stores = [], []
    gathered = {}
    for k in range(chunks):
        for s in range(k * per, (k + 1) * per):
            new = updated(
                mean[s], clip_factor, state[0, s], state[1, s], state[2, s], state[3, s], rates[s // halves]
            )
            for i in range(4):
                fresh[i, s] = new[i]
            for w in range(2):
                half[w, s] = new[w].astype(jnp.bfloat16)
        for w in range(2):
            for b in range(1, nf):
                gathered[k, b, w] = remote(
                    half.at[w, cut[k]], weights[w].at[cut[k], place, :],
                    g_send.at[w, b - 1, k], g_recv.at[w, b - 1, k], fsdp=at_z(b),
                )
                gathered[k, b, w].start()
            for a in range(1, nd):
                spread.append(remote(
                    half.at[w, cut[k]], weights[w].at[cut[k], place, :],
                    f_send.at[w, 0, a - 1, k], f_recv.at[w, 0, a - 1, k], dp=at_x(a),
                ))
                spread[-1].start()
            stores.append(pltpu.make_async_copy(half.at[w, cut[k]], weights[w].at[cut[k], place, :], half_sem.at[w, k]))
            stores[-1].start()
    for i, ref in enumerate((master_out, teacher_out, first_out, second_out)):
        stores.append(pltpu.make_async_copy(fresh.at[i], ref, out_sem.at[i]))
        stores[-1].start()

    for k in range(chunks):
        for b in range(1, nf):
            source = pl.ds(pl.multiple_of((x * nf + lax.rem(z + nf - b, nf)) * rows, rows), rows)
            for w in range(2):
                gathered[k, b, w].wait_recv()
                for a in range(1, nd):
                    there = weights[w].at[cut[k], source, :]
                    spread.append(remote(
                        there, there, f_send.at[w, b, a - 1, k], f_recv.at[w, b, a - 1, k], dp=at_x(a)
                    ))
                    spread[-1].start()
    for copy in stores:
        copy.wait()
    for copy in (*sent.values(), *told, *gathered.values()):
        copy.wait_send()
    for copy in spread:
        copy.wait()


def kernel_shards(sizes, gradients, master, teacher, first_moment, second_moment, layer_rates):
    nd, nf, nm = sizes
    layers, two, rows, width = master.shape
    slabs, full = layers * two, gradients.shape[3]
    chunks = math.gcd(layers, 6)
    shard = (slabs, rows, width)
    f32 = jnp.float32
    anywhere = pl.BlockSpec(memory_space=pl.ANY)
    dma = pltpu.SemaphoreType.DMA
    peers = nd * nf - 1 + nm - 1
    outs = pl.pallas_call(
        functools.partial(step_kernel, sizes, chunks),
        out_shape=[jax.ShapeDtypeStruct(shard, f32)] * 4 + [jax.ShapeDtypeStruct((slabs, full, width), jnp.bfloat16)] * 2,
        in_specs=[anywhere] * 5 + [pl.BlockSpec(memory_space=pltpu.SMEM)],
        out_specs=[anywhere] * 6,
        scratch_shapes=[
            pltpu.VMEM(shard, jnp.bfloat16),
            pltpu.VMEM((nd * nf - 1, *shard), jnp.bfloat16),
            pltpu.VMEM(shard, f32),
            pltpu.VMEM((4, *shard), f32),
            pltpu.VMEM((4, *shard), f32),
            pltpu.VMEM((2, *shard), jnp.bfloat16),
            pltpu.VMEM((2, 8, 128), f32),
            pltpu.VMEM((peers, 8, 128), f32),
            dma((chunks,)), dma((4,)), dma((4,)), dma((2, chunks)),
            dma((nd * nf - 1, chunks)), dma((nd * nf - 1, chunks)),
            dma((peers,)), dma((peers,)),
            dma((2, nf - 1, chunks)), dma((2, nf - 1, chunks)),
            dma((2, nf, nd - 1, chunks)), dma((2, nf, nd - 1, chunks)),
        ],
        compiler_params=pltpu.CompilerParams(
            collective_id=0, has_side_effects=True, vmem_limit_bytes=40 * 1024 * 1024
        ),
    )(
        gradients.reshape(slabs, full, width),
        *(held.reshape(shard) for held in (master, teacher, first_moment, second_moment)),
        layer_rates,
    )
    return tuple(out.reshape(layers, two, *out.shape[1:]) for out in outs)


def shards(sizes, gradients, *rest):
    nd, nf, _ = sizes
    rows, width = rest[0].shape[2:]
    if nd > 1 and nf > 1 and rows % 32 == 0 and width % 128 == 0:
        return kernel_shards(sizes, gradients, *rest)
    return plain_shards(gradients, *rest)


def solution(mesh):
    held = P(None, None, ("dp", "fsdp"), "mp")
    whole = P(None, None, None, "mp")
    sizes = tuple(mesh.shape[axis] for axis in ("dp", "fsdp", "mp"))
    return jax.shard_map(
        functools.partial(shards, sizes),
        mesh=mesh,
        in_specs=(P(("dp", "fsdp"), None, None, None, "mp"), held, held, held, held, P()),
        out_specs=(held, held, held, held, whole, whole),
        check_vma=False,
    )
```

time: 314 us -> 178 us (0.57)
  waiting for transfers between devices: 242 us -> 0 us
  Pallas kernels: 0 us -> 165 us
  blocking collectives: 39.7 us -> 0 us
  between operations: 14.5 us -> 0.66 us
  other arithmetic: 11.7 us -> 0 us
  local copies, waits for them, and re-layouts: 5.69 us -> 12 us
    pallas_call x0 -> x1, Pallas kernels: none -> 165 us  [kernel_shards(): pl.pallas_call(functools.partial(step_kernel, sizes, chunks), out_shape=[...]
    reduce_scatter x1 -> x0, waiting for transfers between devices: 121 us -> none  [shards(): lax.psum_scatter(own_grad, ('dp', 'fsdp'), scatter_dimension=2, tiled=True)]
    all_gather x2 -> x0, waiting for transfers between devices: 120 us -> none  [the longest x1 61.5 us: shards(): lax.all_gather(student_half, ('dp', 'fsdp'), axis=2, tiled=True)]
    psum x1 -> x0, blocking collectives: 39.7 us -> none  [shards(): norm_sq = lax.psum(jnp.sum(mean_grad * mean_grad), ('dp', 'fsdp', 'mp'))]
    convert_element_type x3 -> x0, other arithmetic: 9.8 us -> none  [the longest x1 5.31 us: shards(): own_grad = gradients[0].astype(jnp.float32)]
    unnamed x14 -> x16, local copies, waits for them, and re-layouts: 5.69 us -> 12 us
  transfers between devices with their start and end apart: 3 -> 0, of which waited for: 3 -> 0; matrix products, arithmetic and copies ran while one was open for 0% -> 0% of each run, Pallas kernels for 0% -> 0%
where the time goes in v1:
time: 178 us
  Pallas kernels  165 us (93%)
  local copies, waits for them, and re-layouts  12 us (7%)
    pallas_call x1, Pallas kernels, kernel_shards(): pl.pallas_call(functools.partial(step_kernel, sizes, chunks), out_shape=[...  165 us
    unnamed x16, local copies, waits for them, and re-layouts  12 us

profile of v1, /device:TPU:0, one launch (start us, length us, event | category | flops | bytes accessed | tf_op | source)
XLA Modules:
  0.0 177.8 jit_solution(13738042040751068178)
XLA Ops:
  0.6 0.0 copy-start
  0.6 1.1 copy-done
  1.8 0.0 copy-start.1
  1.8 1.1 copy-done.1
  2.9 0.0 copy-start.2
  2.9 1.1 copy-done.2
  4.0 0.0 copy-start.3
  4.0 1.1 copy-done.3
  5.2 0.0 copy-start.4
  5.2 0.7 copy-done.4
  5.8 165.1 %shard_map.109 = (f32[24,32,256]{2,1,0:T(8,128)S(1)}, f32[24,32,256]{2,1,0:T(8,128)S(1)}, f32[24,32,256]{2,1,0:T(8,128)S(1)}, f32[24,32,256]{2,1,0:T(8,128)S(1)}...) custom-call(bf16[24,256,256]{2,1,0:T(8,128)(2,1)} %bitcast.21, f32[24,32,256]{2,1,0:T(8,128)S(1)} %bitcast.13, ...), custom_call_target="tpu_custom_call" | custom-call | tf_op jit(solution)/shard_map/pallas_call | solution.py:199
  170.9 0.9 copy.18
  171.8 0.9 copy.19
  172.7 0.9 copy.20
  173.6 0.9 copy.21
  174.4 1.7 copy.22
  176.1 1.7 copy.23
Async XLA Ops:
  0.6 1.1 copy-start
  1.8 1.1 copy-start.1
  2.9 1.1 copy-start.2
  4.0 1.1 copy-start.3
  5.2 0.7 copy-start.4

commit v2 on v1

--- a/solution.py
+++ b/solution.py
@@ -48,9 +48,9 @@
 def step_kernel(
     sizes, chunks, grad, master, teacher, first, second, rates,
     master_out, teacher_out, first_out, second_out, student_w, teacher_w,
-    own, met, mean, state, fresh, half, norm_own, norm_met,
-    own_sem, state_sem, out_sem, half_sem,
-    a_send, a_recv, n_send, n_recv, g_send, g_recv, f_send, f_recv,
+    own, met, mean, norm_own, norm_met,
+    own_sem,
+    a_send, a_recv, n_send, n_recv, g_send, g_recv, e_send, e_recv, f_send, f_recv,
 ):
     nd, nf, nm = sizes
     x, z, m = lax.axis_index("dp"), lax.axis_index("fsdp"), lax.axis_index("mp")
@@ -85,7 +85,6 @@
     takes = [pltpu.make_async_copy(grad.at[cut[k], place, :], own.at[cut[k]], own_sem.at[k]) for k in range(chunks)]
     for take in takes:
         take.start()
-    loads = [pltpu.make_async_copy(ref, state.at[i], state_sem.at[i]) for i, ref in enumerate((master, teacher, first, second))]
     pl.semaphore_wait(barrier, len(peers) + nm - 1)
 
     sent = {}
@@ -96,8 +95,6 @@
                 grad.at[cut[k], theirs, :], met.at[i, cut[k]], a_send.at[i, k], a_recv.at[i, k], dp=at_x(a), fsdp=at_z(b)
             )
             sent[k, i].start()
-    for load in loads:
-        load.start()
 
     square = jnp.zeros((8, 128), jnp.float32)
     for k in range(chunks):
@@ -119,8 +116,6 @@
     for i, (a, b) in enumerate(peers):
         told.append(remote(norm_own.at[0], norm_met.at[i], n_send.at[i], n_recv.at[i], dp=at_x(a), fsdp=at_z(b)))
         told[-1].start()
-    for load in loads:
-        load.wait()
     for i in range(len(peers)):
         told[i].wait_recv()
         square = square + norm_met[i]
@@ -137,53 +132,109 @@
     clip_factor = jnp.minimum(1.0, CLIP_NORM / (jnp.sqrt(norm_sq) + 1e-06))
 
     weights = (student_w, teacher_w)
-    spread, stores = [], []
-    gathered = {}
+    news = (master_out, teacher_out, first_out, second_out)
+    last = nf - 1
+
+    def bands(k, column, row):
+        return [ref.at[cut[k], pl.ds(pl.multiple_of((column * nf + row) * rows, rows), rows), :] for ref in weights]
+
+    def along(way, k, d):
+        there = bands(k, x, z - d if way == 0 else z + d)
+        return [
+            remote(there[w], there[w], g_send.at[way, w, d, k], g_recv.at[way, w, d, k], fsdp=z + 1 if way == 0 else z - 1)
+            for w in range(2)
+        ]
+
+    def arriving(way, k, d):
+        there = bands(k, x, z - d if way == 0 else z + d)
+        return [remote(there[w], there[w], g_send.at[way, w, d, k], g_recv.at[way, w, d - 1, k], fsdp=z) for w in range(2)]
+
+    def far(way, k):
+        there = bands(k, 1 - x, 0 if way == 0 else last)
+        return [
+            remote(there[w], there[w], e_send.at[way, w, k], e_recv.at[way, w, k], fsdp=z + 1 if way == 0 else z - 1)
+            for w in range(2)
+        ]
+
+    def across(way, k, d):
+        there = bands(k, x, z - d if way == 0 else z + d)
+        return [
+            remote(there[w], there[w], f_send.at[way, w, d, k], f_recv.at[way, w, d, k], dp=1 - x) for w in range(2)
+        ]
+
+    def start(copies):
+        for copy in copies:
+            copy.start()
+
+    def wait_recv(copies):
+        for copy in copies:
+            copy.wait_recv()
+
+    def wait_send(copies):
+        for copy in copies:
+            copy.wait_send()
+
+    inner = (z < last, z > 0)
+    origin = (z == 0, z == last)
+
+    def has(way, d):
+        return z >= d if way == 0 else z + d <= last
+
+    def crosses(way, k, d):
+        from_end = z == d if way == 0 else z + d == last
+        return jnp.logical_and(has(way, d), jnp.logical_not(from_end)) if k % 2 else has(way, d)
+
     for k in range(chunks):
         for s in range(k * per, (k + 1) * per):
             new = updated(
-                mean[s], clip_factor, state[0, s], state[1, s], state[2, s], state[3, s], rates[s // halves]
+                mean[s], clip_factor, master[s], teacher[s], first[s], second[s], rates[s // halves]
             )
             for i in range(4):
-                fresh[i, s] = new[i]
+                news[i][s] = new[i]
             for w in range(2):
-                half[w, s] = new[w].astype(jnp.bfloat16)
-        for w in range(2):
-            for b in range(1, nf):
-                gathered[k, b, w] = remote(
-                    half.at[w, cut[k]], weights[w].at[cut[k], place, :],
-                    g_send.at[w, b - 1, k], g_recv.at[w, b - 1, k], fsdp=at_z(b),
-                )
-                gathered[k, b, w].start()
-            for a in range(1, nd):
-                spread.append(remote(
-                    half.at[w, cut[k]], weights[w].at[cut[k], place, :],
-                    f_send.at[w, 0, a - 1, k], f_recv.at[w, 0, a - 1, k], dp=at_x(a),
-                ))
-                spread[-1].start()
-            stores.append(pltpu.make_async_copy(half.at[w, cut[k]], weights[w].at[cut[k], place, :], half_sem.at[w, k]))
-            stores[-1].start()
-    for i, ref in enumerate((master_out, teacher_out, first_out, second_out)):
-        stores.append(pltpu.make_async_copy(fresh.at[i], ref, out_sem.at[i]))
-        stores[-1].start()
-
-    for k in range(chunks):
-        for b in range(1, nf):
-            source = pl.ds(pl.multiple_of((x * nf + lax.rem(z + nf - b, nf)) * rows, rows), rows)
-            for w in range(2):
-                gathered[k, b, w].wait_recv()
-                for a in range(1, nd):
-                    there = weights[w].at[cut[k], source, :]
-                    spread.append(remote(
-                        there, there, f_send.at[w, b, a - 1, k], f_recv.at[w, b, a - 1, k], dp=at_x(a)
-                    ))
-                    spread[-1].start()
-    for copy in stores:
-        copy.wait()
-    for copy in (*sent.values(), *told, *gathered.values()):
+                weights[w][s, place, :] = new[w].astype(jnp.bfloat16)
+        start(across(0, k, 0))
+        for way in range(2):
+            pl.when(inner[way])(lambda way=way: start(along(way, k, 0)))
+
+    odd = range(1, chunks, 2)
+    for k in odd:
+        wait_recv(across(0, k, 0))
+        for way in range(2):
+            pl.when(origin[way])(lambda way=way, k=k: start(far(way, k)))
+    for d in range(1, nf):
+        for k in range(chunks):
+            for way in range(2):
+                @pl.when(has(way, d))
+                def _(way=way, d=d, k=k):
+                    wait_recv(arriving(way, k, d))
+                    pl.when(inner[way])(lambda: start(along(way, k, d)))
+                    pl.when(crosses(way, k, d))(lambda: start(across(way, k, d)))
+        for k in odd:
+            for way in range(2):
+                @pl.when(z == d if way == 0 else z == last - d)
+                def _(way=way, k=k):
+                    wait_recv(far(way, k))
+                    pl.when(inner[way])(lambda: start(far(way, k)))
+
+    for copy in (*sent.values(), *told):
         copy.wait_send()
-    for copy in spread:
-        copy.wait()
+    for k in range(chunks):
+        if k % 2 == 0:
+            wait_recv(across(0, k, 0))
+        wait_send(across(0, k, 0))
+        for way in range(2):
+            for d in range(nf):
+                @pl.when(jnp.logical_and(has(way, d), inner[way]))
+                def _(way=way, d=d, k=k):
+                    wait_send(along(way, k, d))
+                if d:
+                    @pl.when(crosses(way, k, d))
+                    def _(way=way, d=d, k=k):
+                        wait_recv(across(way, k, d))
+                        wait_send(across(way, k, d))
+            if k % 2:
+                pl.when(inner[way])(lambda way=way, k=k: wait_send(far(way, k)))
 
 
 def kernel_shards(sizes, gradients, master, teacher, first_moment, second_moment, layer_rates):
@@ -193,28 +244,27 @@
     chunks = math.gcd(layers, 6)
     shard = (slabs, rows, width)
     f32 = jnp.float32
-    anywhere = pl.BlockSpec(memory_space=pl.ANY)
+    outside = pl.BlockSpec(memory_space=pltpu.HBM)
+    inside = pl.BlockSpec(memory_space=pltpu.VMEM)
     dma = pltpu.SemaphoreType.DMA
     peers = nd * nf - 1 + nm - 1
     outs = pl.pallas_call(
         functools.partial(step_kernel, sizes, chunks),
         out_shape=[jax.ShapeDtypeStruct(shard, f32)] * 4 + [jax.ShapeDtypeStruct((slabs, full, width), jnp.bfloat16)] * 2,
-        in_specs=[anywhere] * 5 + [pl.BlockSpec(memory_space=pltpu.SMEM)],
-        out_specs=[anywhere] * 6,
+        in_specs=[outside] + [inside] * 4 + [pl.BlockSpec(memory_space=pltpu.SMEM)],
+        out_specs=[inside] * 6,
         scratch_shapes=[
             pltpu.VMEM(shard, jnp.bfloat16),
             pltpu.VMEM((nd * nf - 1, *shard), jnp.bfloat16),
             pltpu.VMEM(shard, f32),
-            pltpu.VMEM((4, *shard), f32),
-            pltpu.VMEM((4, *shard), f32),
-            pltpu.VMEM((2, *shard), jnp.bfloat16),
             pltpu.VMEM((2, 8, 128), f32),
             pltpu.VMEM((peers, 8, 128), f32),
-            dma((chunks,)), dma((4,)), dma((4,)), dma((2, chunks)),
+            dma((chunks,)),
             dma((nd * nf - 1, chunks)), dma((nd * nf - 1, chunks)),
             dma((peers,)), dma((peers,)),
-            dma((2, nf - 1, chunks)), dma((2, nf - 1, chunks)),
-            dma((2, nf, nd - 1, chunks)), dma((2, nf, nd - 1, chunks)),
+            dma((2, 2, nf, chunks)), dma((2, 2, nf, chunks)),
+            dma((2, 2, chunks)), dma((2, 2, chunks)),
+            dma((2, 2, nf, chunks)), dma((2, 2, nf, chunks)),
         ],
         compiler_params=pltpu.CompilerParams(
             collective_id=0, has_side_effects=True, vmem_limit_bytes=40 * 1024 * 1024
@@ -230,7 +280,7 @@
 def shards(sizes, gradients, *rest):
     nd, nf, _ = sizes
     rows, width = rest[0].shape[2:]
-    if nd > 1 and nf > 1 and rows % 32 == 0 and width % 128 == 0:
+    if nd == 2 and nf > 1 and rows % 32 == 0 and width % 128 == 0:
         return kernel_shards(sizes, gradients, *rest)
     return plain_shards(gradients, *rest)
 

time: 178 us -> 164 us (0.921)
  Pallas kernels: 165 us -> 151 us
    pallas_call x1, Pallas kernels: 165 us -> 151 us  [kernel_shards(): pl.pallas_call(functools.partial(step_kernel, sizes, chunks), out_shape=[...]
where the time goes in v2:
time: 164 us
  Pallas kernels  151 us (92%)
  local copies, waits for them, and re-layouts  12 us (7%)
    pallas_call x1, Pallas kernels, kernel_shards(): pl.pallas_call(functools.partial(step_kernel, sizes, chunks), out_shape=[...  151 us
    unnamed x16, local copies, waits for them, and re-layouts  12 us

profile of v2, /device:TPU:0, one launch (start us, length us, event | category | flops | bytes accessed | tf_op | source)
XLA Modules:
  0.0 163.5 jit_solution(5665473578220518213)
XLA Ops:
  0.6 0.0 copy-start
  0.6 1.1 copy-done
  1.8 0.0 copy-start.1
  1.8 1.1 copy-done.1
  2.9 0.0 copy-start.2
  2.9 1.1 copy-done.2
  4.0 0.0 copy-start.3
  4.0 1.1 copy-done.3
  5.2 0.0 copy-start.4
  5.2 0.7 copy-done.4
  5.8 150.8 %shard_map.109 = (f32[24,32,256]{2,1,0:T(8,128)S(1)}, f32[24,32,256]{2,1,0:T(8,128)S(1)}, f32[24,32,256]{2,1,0:T(8,128)S(1)}, f32[24,32,256]{2,1,0:T(8,128)S(1)}...) custom-call(bf16[24,256,256]{2,1,0:T(8,128)(2,1)} %bitcast.21, f32[24,32,256]{2,1,0:T(8,128)S(1)} %bitcast.13, ...), custom_call_target="tpu_custom_call" | custom-call | tf_op jit(solution)/shard_map/pallas_call | solution.py:251
  156.7 0.9 copy.18
  157.6 0.9 copy.19
  158.4 0.9 copy.20
  159.3 0.9 copy.21
  160.2 1.7 %copy.22 = bf16[12,2,256,256]{3,2,1,0:T(8,128)(2,1)} copy(bf16[12,2,256,256]{3,2,1,0:T(8,128)(2,1)S(1)} %bitcast.12) | data formatting | bytes 6291456
  161.9 1.7 %copy.23 = bf16[12,2,256,256]{3,2,1,0:T(8,128)(2,1)} copy(bf16[12,2,256,256]{3,2,1,0:T(8,128)(2,1)S(1)} %bitcast.11) | data formatting | bytes 6291456
Async XLA Ops:
  0.6 1.1 copy-start
  1.8 1.1 copy-start.1
  2.9 1.1 copy-start.2
  4.0 1.1 copy-start.3
  5.2 0.7 copy-start.4
